TPU v7x, 32 devices: a whole 2x2x4 slice. The times are simulated.
32 devices in a mesh: dp: 8 (over y, x, core), tensor: 4 (over z).
Axes of the slice: x: 2, y: 2, z: 4, core: 2. Of those that a mesh axis runs over, the one named last changes fastest.
Arguments:
- img_hidden: bfloat16 [4096, 4304], P('dp', 'tensor'), may hold values from -0.25 to 0.25
- img_down: bfloat16 [4304, 1152], P('tensor'), may hold values from -0.09375 to 0.09375
- img_pooled: bfloat16 [4096, 1152], P(('dp', 'tensor')), may hold values from -0.25 to 0.25
- txt_hidden: bfloat16 [4096, 1152], P('dp', 'tensor'), may hold values from -0.25 to 0.25
- txt_proj: bfloat16 [1152, 1152], P('tensor'), may hold values from -0.1875 to 0.1875
- log_temp: float32 [1], replicated, may hold values from 1 to 2
- bias: float32 [1], replicated, may hold values from -4 to -1
- match: int32 [4096], P(('dp', 'tensor')), may hold values from 0 to 4095
- window_index: int32 [1], replicated, may hold values from 0 to 1
Outputs:
- img_grad: float32 [4096, 1152], P(('dp', 'tensor'))
- txt_grad: float32 [4096, 1152], P(('dp', 'tensor'))
- row_loss: float32 [4096], P(('dp', 'tensor'))
All inputs are finite; a program needn't handle non-finite values.
Results may differ from a plain program's by a relative error of at most 0.0039.
Values may be sent and summed in bfloat16 or wider, within the bound.
A program may use at most 64 MiB of HBM per device.

v0:
```python
import jax
import jax.numpy as jnp
from jax import lax
from jax.experimental import pallas as pl
from jax.experimental.pallas import tpu as pltpu
from jax.sharding import PartitionSpec as P

STEPS = 16


def shifted(shard, axis, by):
    devices = lax.axis_size(axis)
    return lax.ppermute(shard, axis, [(i, (i + by) % devices) for i in range(devices)])


def unit_rows(emb):
    length = jnp.sqrt(jnp.sum(emb * emb, axis=1, keepdims=True) + 1e-06)
    return (emb / length, length)


def pair_tile(image_low, text_block, owner, match, scale, shift_value):
    cosine = lax.dot_general(
        image_low, text_block, (((1,), (1,)), ((), ())), preferred_element_type=jnp.float32
    )
    text_index = owner * text_block.shape[0] + lax.iota(jnp.int32, text_block.shape[0])
    positive = match[:, None] == text_index[None, :]
    logit = scale * cosine + shift_value
    pair_loss = jnp.sum(
        jnp.where(positive, jax.nn.softplus(-logit), jax.nn.softplus(logit)), axis=1
    )
    coef = ((jax.nn.sigmoid(logit) - positive.astype(jnp.float32)) * scale).astype(jnp.bfloat16)
    image_part = jnp.dot(coef, text_block, preferred_element_type=jnp.float32)
    text_part = lax.dot_general(
        coef, image_low, (((0,), (0,)), ((), ())), preferred_element_type=jnp.float32
    )
    return (pair_loss, image_part, text_part)


def offset_blocks(blocks, window):
    windows = lax.axis_size(("dp", "tensor")) // STEPS
    for level in range((windows - 1).bit_length()):
        moved = shifted(blocks, ("dp", "tensor"), STEPS << level)
        blocks = jnp.where(window >> level & 1 == 1, moved, blocks)
    return blocks


def return_home(text_sum, fixed_steps, window):
    text_sum = shifted(text_sum, ("dp", "tensor"), -fixed_steps)
    windows = lax.axis_size(("dp", "tensor")) // STEPS
    for level in range((windows - 1).bit_length()):
        moved = shifted(text_sum, ("dp", "tensor"), -(STEPS << level))
        text_sum = jnp.where(window >> level & 1 == 1, moved, text_sum)
    return text_sum


def ring_body(
    img_hidden, img_down, img_pooled, txt_hidden, txt_proj, log_temp, bias, match, window_index
):
    width = img_pooled.shape[1]
    summed = lax.psum_scatter(
        jnp.concatenate(
            [
                jnp.dot(img_hidden, img_down, preferred_element_type=jnp.float32),
                jnp.dot(txt_hidden, txt_proj, preferred_element_type=jnp.float32),
            ],
            axis=1,
        ),
        "tensor",
        scatter_dimension=0,
        tiled=True,
    )
    img_emb = summed[:, :width] + img_pooled.astype(jnp.float32)
    txt_emb = summed[:, width:]
    img_unit, img_len = unit_rows(img_emb)
    txt_unit, txt_len = unit_rows(txt_emb)
    image_low = img_unit.astype(jnp.bfloat16)
    text_low = txt_unit.astype(jnp.bfloat16)
    scale = jnp.exp(log_temp[0])
    shift_value = bias[0]
    window = window_index[0]
    start_step = window * STEPS
    position = lax.axis_index(("dp", "tensor"))
    devices = lax.axis_size(("dp", "tensor"))
    half_steps = STEPS // 2
    late_copy = shifted(text_low, ("dp", "tensor"), STEPS - 1)
    stacked = offset_blocks(jnp.stack([text_low, late_copy]), window)
    early_block = stacked[0]
    late_block = stacked[1]
    early_owner = (position - start_step) % devices
    late_owner = (position - start_step - (STEPS - 1)) % devices
    early_loss, early_image, early_sum = pair_tile(
        image_low, early_block, early_owner, match, scale, shift_value
    )
    late_loss, late_image, late_sum = pair_tile(
        image_low, late_block, late_owner, match, scale, shift_value
    )

    def two_turn(turn, carry):
        early_now, late_now, early_acc, late_acc, image_now, loss_now = carry
        early_now = shifted(early_now, ("dp", "tensor"), 1)
        late_now = shifted(late_now, ("dp", "tensor"), -1)
        early_acc = shifted(early_acc, ("dp", "tensor"), 1)
        late_acc = shifted(late_acc, ("dp", "tensor"), -1)
        owner_early = (position - start_step - turn) % devices
        owner_late = (position - start_step - (STEPS - 1) + turn) % devices
        loss_one, image_one, text_one = pair_tile(
            image_low, early_now, owner_early, match, scale, shift_value
        )
        loss_two, image_two, text_two = pair_tile(
            image_low, late_now, owner_late, match, scale, shift_value
        )
        return (
            early_now,
            late_now,
            early_acc + text_one,
            late_acc + text_two,
            image_now + image_one + image_two,
            loss_now + loss_one + loss_two,
        )

    carried = lax.fori_loop(
        1,
        half_steps,
        two_turn,
        (
            early_block,
            late_block,
            early_sum,
            late_sum,
            early_image + late_image,
            early_loss + late_loss,
        ),
    )
    early_sum = carried[2]
    late_sum = carried[3]
    image_dunit = carried[4]
    row_loss = carried[5]
    late_moved = shifted(late_sum, ("dp", "tensor"), -1)
    text_dunit = return_home(early_sum + late_moved, half_steps - 1, window)
    img_grad = (
        image_dunit - img_unit * jnp.sum(img_unit * image_dunit, axis=1, keepdims=True)
    ) / img_len
    txt_grad = (
        text_dunit - txt_unit * jnp.sum(txt_unit * text_dunit, axis=1, keepdims=True)
    ) / txt_len
    return (img_grad, txt_grad, row_loss)


def scatter_sum(partial, axis):
    parts = lax.axis_size(axis)
    rows = partial.shape[0] // parts
    pieces = partial.astype(jnp.bfloat16).reshape(parts, rows, partial.shape[1])
    got = lax.all_to_all(pieces, axis, 0, 0).astype(jnp.float32)
    return jnp.sum(got, axis=0)


def stable_terms(logit, positive):
    signed = jnp.where(positive, -logit, logit)
    small = jnp.exp(-jnp.abs(signed))
    loss = jnp.maximum(signed, 0.0) + jnp.log1p(small)
    chance = jnp.where(signed >= 0.0, 1.0, small) / (1.0 + small)
    return loss, jnp.where(positive, -chance, chance)


def tangent(dunit, unit, length):
    return (dunit - unit * jnp.sum(unit * dunit, axis=1, keepdims=True)) / length


def exchange(pay, out, twin, col, z_send, z_recv, p_send, f_send, out_recv, twin_recv, local_sem):
    dp = lax.axis_index("dp")
    z = lax.axis_index("tensor")
    depth = lax.axis_size("tensor")
    devices = lax.axis_size("dp") * depth
    half = devices // 2
    y, x, c = dp // 4, (dp // 2) % 2, dp % 2

    def group(y, x, c):
        return y * 4 + x * 2 + c

    def slot(kind, source, target):
        ahead = (1 - 2 * kind) * (target - source)
        return kind * (half - 1) + lax.rem(ahead + devices, devices) - 1

    peers = [
        group(y, x, 1 - c),
        group(y, 1 - x, c),
        group(1 - y, 1 - x, c),
        group(1 - y, x, 1 - c),
        group(1 - y, x, c),
    ]
    barrier = pltpu.get_barrier_semaphore()
    for peer in peers:
        pl.semaphore_signal(barrier, inc=1, device_id=(peer, z), device_id_type=pl.DeviceIdType.MESH)
    has_up = z < depth - 1
    has_down = z > 0

    @pl.when(has_up)
    def _():
        pl.semaphore_signal(barrier, inc=1, device_id=(dp, z + 1), device_id_type=pl.DeviceIdType.MESH)

    @pl.when(has_down)
    def _():
        pl.semaphore_signal(barrier, inc=1, device_id=(dp, z - 1), device_id_type=pl.DeviceIdType.MESH)

    inner = jnp.logical_and(has_up, has_down)

    @pl.when(inner)
    def _():
        pl.semaphore_wait(barrier, len(peers) + 2)

    @pl.when(jnp.logical_not(inner))
    def _():
        pl.semaphore_wait(barrier, len(peers) + 1)

    started = []

    def start(condition, make):
        @pl.when(condition)
        def _():
            make().start()

        started.append((condition, make))

    def remote(source, target, send, recv, peer, level):
        return lambda: pltpu.make_async_remote_copy(
            src_ref=source(),
            dst_ref=target(),
            send_sem=send(),
            recv_sem=recv(),
            device_id=(peer, level),
            device_id_type=pl.DeviceIdType.MESH,
        )

    def arrived(condition, index):
        @pl.when(condition)
        def _():
            pltpu.make_async_remote_copy(
                src_ref=out.at[index],
                dst_ref=out.at[index],
                send_sem=f_send.at[0, 0],
                recv_sem=out_recv.at[index],
                device_id=(peers[0], z),
                device_id_type=pl.DeviceIdType.MESH,
            ).wait_recv()

    def along(tag, level, kind, way, condition):
        held = (lambda: pay.at[kind]) if tag == 0 else (lambda: col.at[level, kind])
        start(
            condition,
            remote(
                held,
                lambda: col.at[level, kind],
                lambda: z_send.at[tag, kind, way],
                lambda: z_recv.at[level, kind],
                dp,
                z + 1 - 2 * way,
            ),
        )

    def spread(tag, level, condition):
        source = dp * depth + level

        def send(job, kind, peer, when):
            index = slot(kind, source, peer * depth + z)
            held = (lambda: pay.at[kind]) if tag == 0 else (lambda: col.at[level, kind])
            start(
                when,
                remote(
                    held,
                    lambda: out.at[index],
                    lambda: p_send.at[tag, job],
                    lambda: out_recv.at[index],
                    peer,
                    z,
                ),
            )

        send(0, 1 - c, peers[3], condition)
        send(1, 1 - x, peers[2], condition)
        send(2, x, peers[1], condition)
        send(3, c, peers[0], condition)
        if tag == 0:
            for kind in (0, 1):
                start(
                    condition,
                    remote(
                        lambda kind=kind: pay.at[kind],
                        lambda kind=kind: twin.at[kind],
                        lambda kind=kind: p_send.at[0, 4 + kind],
                        lambda kind=kind: twin_recv.at[kind],
                        peers[4],
                        z,
                    ),
                )
        else:
            below = tag % 2
            send(4, c, peers[4], jnp.logical_and(condition, c == below))

    def keep(tag, level, condition):
        kind = 1 - tag % 2
        index = slot(kind, dp * depth + level, dp * depth + z)

        @pl.when(condition)
        def _():
            pltpu.make_async_copy(col.at[level, kind], out.at[index], local_sem.at[tag]).start()

    def kept(tag, level, condition):
        kind = 1 - tag % 2
        index = slot(kind, dp * depth + level, dp * depth + z)

        @pl.when(condition)
        def _():
            pltpu.make_async_copy(col.at[level, kind], out.at[index], local_sem.at[tag]).wait()

    def relay(tag, level, condition):
        me = dp * depth + z
        other = peers[0] * depth + z

        def hand(job, kind, origin, when, onward):
            source = origin * depth + level
            arrived(when, slot(kind, source, me))
            if onward is not None:
                index = slot(kind, source, me)
                landing = slot(kind, source, other)
                start(
                    onward,
                    remote(
                        lambda: out.at[index],
                        lambda: out.at[landing],
                        lambda: f_send.at[tag, job],
                        lambda: out_recv.at[landing],
                        peers[0],
                        z,
                    ),
                )

        hand(0, 1 - x, peers[1], condition, condition)
        hand(1, x, peers[2], condition, condition)
        onward = None if tag == 0 else jnp.logical_and(condition, c == tag % 2)
        hand(2, c, peers[3], condition, onward)

    def finish(tag, level, condition):
        me = dp * depth + z
        arrived(condition, slot(1 - c, peers[0] * depth + level, me))
        arrived(condition, slot(1 - x, group(y, 1 - x, 1 - c) * depth + level, me))
        arrived(condition, slot(x, group(1 - y, 1 - x, 1 - c) * depth + level, me))
        if tag:
            arrived(condition, slot(tag % 2, peers[4] * depth + level, me))

    always = z >= 0
    for kind in (0, 1):
        along(0, z, kind, 0, has_up)
        along(0, z, kind, 1, has_down)
    spread(0, z, always)
    turns = [(0, z, always)]
    for hop in range(1, depth):
        here = []
        for way in (0, 1):
            level = z - hop if way == 0 else z + hop
            condition = level >= 0 if way == 0 else level < depth
            tag = 2 * hop - 1 if way == 0 else 2 * hop
            for kind in (0, 1):

                @pl.when(condition)
                def _():
                    pltpu.make_async_remote_copy(
                        src_ref=col.at[level, kind],
                        dst_ref=col.at[level, kind],
                        send_sem=f_send.at[0, 0],
                        recv_sem=z_recv.at[level, kind],
                        device_id=(peers[0], z),
                        device_id_type=pl.DeviceIdType.MESH,
                    ).wait_recv()

                if hop < depth - 1:
                    more = has_up if way == 0 else has_down
                    along(tag, level, kind, way, jnp.logical_and(condition, more))
            spread(tag, level, condition)
            keep(tag, level, condition)
            here.append((tag, level, condition))
        for turn in turns[-2 if hop > 1 else -1 :]:
            relay(*turn)
        turns += here
    for turn in turns[-2:]:
        relay(*turn)
    for turn in turns:
        finish(*turn)
        if turn[0]:
            kept(*turn)
    for kind in (0, 1):
        pltpu.make_async_remote_copy(
            src_ref=twin.at[kind],
            dst_ref=twin.at[kind],
            send_sem=f_send.at[0, 0],
            recv_sem=twin_recv.at[kind],
            device_id=(peers[4], z),
            device_id_type=pl.DeviceIdType.MESH,
        ).wait_recv()
    for condition, make in started:

        @pl.when(condition)
        def _():
            make().wait_send()


def swap_blocks(pay):
    devices = lax.axis_size(("dp", "tensor"))
    depth = lax.axis_size("tensor")
    slots = devices - 2
    tags = 2 * depth - 1
    block = pay.shape[1:]
    dma = pltpu.SemaphoreType.DMA
    return pl.pallas_call(
        exchange,
        out_shape=(
            jax.ShapeDtypeStruct((slots,) + block, pay.dtype),
            jax.ShapeDtypeStruct((2,) + block, pay.dtype),
        ),
        in_specs=[pl.BlockSpec(memory_space=pltpu.VMEM)],
        out_specs=(pl.BlockSpec(memory_space=pl.ANY), pl.BlockSpec(memory_space=pl.ANY)),
        scratch_shapes=[
            pltpu.VMEM((depth, 2) + block, pay.dtype),
            dma((tags, 2, 2)),
            dma((depth, 2)),
            dma((tags, 6)),
            dma((tags, 3)),
            dma((slots,)),
            dma((2,)),
            dma((tags,)),
        ],
        compiler_params=pltpu.CompilerParams(collective_id=1, has_side_effects=True),
    )(pay)


def gather_body(
    img_hidden, img_down, img_pooled, txt_hidden, txt_proj, log_temp, bias, match, window_index
):
    both = ("dp", "tensor")
    width = img_pooled.shape[1]
    rows = img_pooled.shape[0]
    devices = lax.axis_size(both)
    position = lax.axis_index(both)
    txt_emb = scatter_sum(jnp.dot(txt_hidden, txt_proj, preferred_element_type=jnp.float32), "tensor")
    img_emb = scatter_sum(
        jnp.dot(img_hidden, img_down, preferred_element_type=jnp.float32), "tensor"
    ) + img_pooled.astype(jnp.float32)
    img_unit, img_len = unit_rows(img_emb)
    txt_unit, txt_len = unit_rows(txt_emb)
    image_low = img_unit.astype(jnp.bfloat16)
    text_low = txt_unit.astype(jnp.bfloat16)
    matches = lax.all_gather(match, both, axis=0, tiled=True).reshape(devices, rows)
    scale = jnp.exp(log_temp[0])
    shift_value = bias[0]
    first = window_index[0] == 0
    pay = jnp.where(first, jnp.stack([text_low, image_low]), jnp.stack([image_low, text_low]))
    slots, twin = swap_blocks(pay)
    count = devices // 2 - 1
    start = jnp.where(first, pay, twin)
    away = jnp.where(first, 0, devices // 2)
    own = position * rows + lax.iota(jnp.int32, rows)
    steps = 1 + lax.iota(jnp.int32, count)

    def side(kind, left, sign, texts_here):
        far = slots[kind * count : (kind + 1) * count].reshape(count * rows, -1)
        near = start[kind]
        owners = jnp.concatenate([(position + away)[None], position - sign * steps]) % devices
        columns = (owners[:, None] * rows + lax.iota(jnp.int32, rows)[None, :]).reshape(-1)
        wanted = jnp.where(texts_here, match, own)
        offered = jnp.where(texts_here, columns, matches[owners].reshape(-1))
        nt = (((1,), (1,)), ((), ()))

        def part(block, offered):
            cosine = lax.dot_general(left, block, nt, preferred_element_type=jnp.float32)
            logit = scale * cosine + shift_value
            loss, slope = stable_terms(logit, wanted[:, None] == offered[None, :])
            coef = (slope * scale).astype(jnp.bfloat16)
            return jnp.sum(loss, axis=1), jnp.dot(coef, block, preferred_element_type=jnp.float32)

        near_loss, near_sum = part(near, offered[:rows])
        far_loss, far_sum = part(far, offered[rows:])
        return near_loss + far_loss, near_sum + far_sum

    loss_a, sum_a = side(0, pay[1], 1, first)
    loss_b, sum_b = side(1, pay[0], -1, jnp.logical_not(first))
    return (
        tangent(jnp.where(first, sum_a, sum_b), img_unit, img_len),
        tangent(jnp.where(first, sum_b, sum_a), txt_unit, txt_len),
        jnp.where(first, loss_a, loss_b),
    )


def solution(mesh):
    in_specs = (
        P("dp", "tensor"),
        P("tensor", None),
        P(("dp", "tensor"), None),
        P("dp", "tensor"),
        P("tensor", None),
        P(),
        P(),
        P(("dp", "tensor")),
        P(),
    )
    out_specs = (P(("dp", "tensor"), None), P(("dp", "tensor"), None), P(("dp", "tensor")))
    whole = mesh.shape["dp"] * mesh.shape["tensor"]
    body = gather_body if whole == 2 * STEPS and mesh.shape["dp"] == 8 else ring_body
    return jax.shard_map(body, mesh=mesh, in_specs=in_specs, out_specs=out_specs, check_vma=False)
```

profile of v0, /device:TPU:0, one launch (start us, length us, event | category | flops | bytes accessed | tf_op | source)
XLA Modules:
  0.0 231.2 jit_solution(10114212178739413873)
XLA Ops:
  0.6 0.0 copy-start
  0.6 0.0 copy-start.9
  0.7 1.7 copy-done
  2.3 4.1 %convolution_convert_fusion = bf16[512,1152]{1,0:T(8,128)(2,1)} fusion(bf16[512,1076]{0,1:T(8,128)(2,1)} %param.9, bf16[1076,1152]{1,0:T(8,128)(2,1)S(1)} %copy-done), kind=kOutput, calls=%fused_computation.2 | convolution fusion | flops 1269891072 | bytes 4760576 | tf_op jit(solution)/shard_map/dot_general | solution.py:445
  6.5 6.5 %all-to-all-start.1 = ((bf16[4,128,1152]{2,1,0:T(8,128)(2,1)}), bf16[4,128,1152]{2,1,0:T(8,128)(2,1)}, u32[]{:S(2)}, u32[]{:S(2)}) async-start(bf16[4,128,1152]{2,1,0:T(8,128)(2,1)} %bitcast.87), calls=%async_computation.1 | async-start | bytes 2359296 | tf_op jit(solution)/shard_map/all_to_all | solution.py:153
  13.6 0.0 copy-done.9
  13.6 84.9 %all-gather = s32[32,1,128]{2,1,0:T(1,128)S(1)} all-gather(s32[1,1,128]{2,1,0:T(1,128)S(1)} %bitcast.89), channel_id=1, replica_groups=mesh['dp'=8,'tensor'=4] {'dp','tensor'}, dimensions={0}, use_global_device_ids=true | all-gather | bytes 16896 | tf_op jit(solution)/shard_map/all_gather | solution.py:451
  98.5 0.1 fusion.47
  98.6 0.6 gather_fusion.1
  99.2 0.1 fusion.46
  99.3 0.6 gather_fusion
  99.9 0.1 fusion.41
  99.9 0.1 fusion.40
  100.0 0.1 add_select_fusion.1
  100.1 0.1 add_select_fusion
  100.2 0.0 copy-done.10
  100.2 3.0 %convolution_convert_fusion.1 = bf16[512,1152]{1,0:T(8,128)(2,1)} fusion(bf16[512,288]{0,1:T(8,128)(2,1)S(1)} %copy-done.10, bf16[288,1152]{1,0:T(8,128)(2,1)} %param.13), kind=kOutput, calls=%fused_computation.3 | convolution fusion | flops 340328448 | bytes 2138112 | tf_op jit(solution)/shard_map/dot_general | solution.py:443
  103.2 0.0 all-to-all-done.1
  103.2 4.4 %all-to-all-start = ((bf16[4,128,1152]{2,1,0:T(8,128)(2,1)}), bf16[4,128,1152]{2,1,0:T(8,128)(2,1)}, u32[]{:S(2)}, u32[]{:S(2)}) async-start(bf16[4,128,1152]{2,1,0:T(8,128)(2,1)} %bitcast.88), calls=%async_computation | async-start | bytes 2359296 | tf_op jit(solution)/shard_map/all_to_all | solution.py:153
  109.0 1.5 convert_reduce_fusion
  110.5 0.0 copy-done.3
  110.5 0.2 multiply_reduce_fusion.2
  110.7 0.8 convert_bitcast_fusion
  111.5 20.4 %all-to-all-done = bf16[4,128,1152]{2,1,0:T(8,128)(2,1)} async-done(((bf16[4,128,1152]{2,1,0:T(8,128)(2,1)}), bf16[4,128,1152]{2,1,0:T(8,128)(2,1)}, u32[]{:S(2)}, u32[]{:S(2)}) %all-to-all-start) | async-done | bytes 1179680 | tf_op jit(solution)/shard_map/all_to_all | solution.py:153
  131.9 1.5 convert_reduce_fusion.1
  133.4 0.0 copy-start.1
  133.5 0.1 multiply_reduce_fusion.3
  133.6 0.7 copy-done.1
  134.3 0.1 fusion.8
  134.4 0.0 copy-start.4
  134.4 0.7 copy-done.4
  135.1 0.9 maximum_select_fusion.pay
  136.0 78.2 %shard_map.112 = (bf16[30,128,1152]{2,1,0:T(8,128)(2,1)}, bf16[2,128,1152]{2,1,0:T(8,128)(2,1)}) custom-call(bf16[2,128,1152]{2,1,0:T(8,128)(2,1)} %maximum_select_fusion.pay), custom_call_target="tpu_custom_call" | custom-call | tf_op jit(solution)/shard_map/pallas_call | solution.py:413
  214.2 0.0 copy-start.6
  214.2 1.4 broadcast_select_fusion
  215.7 1.3 add_reduce_fusion.2
  216.9 1.2 fusion.23
  218.2 0.3 add_reduce_fusion.3
  218.5 1.1 fusion.22
  219.6 4.1 %fusion.59 = (bf16[15,128,1152]{2,1,0:T(8,128)(2,1)S(1)}, bf16[15,128,1152]{2,1,0:T(8,128)(2,1)S(1)}) fusion(bf16[30,128,1152]{2,1,0:T(8,128)(2,1)} %get-tuple-element.6), kind=kLoop, calls=%fused_computation.131 | loop fusion | bytes 17694720 | tf_op jit(solution)/shard_map/slice | solution.py:464
  223.8 0.0 copy-start.8
  223.8 1.6 add_reduce_fusion.1
  225.4 1.1 convolution_add_fusion.1
  226.5 0.0 copy-start.2
  226.5 1.6 add_reduce_fusion
  228.2 1.2 multiply_reduce_fusion
  229.4 1.3 subtract_divide_fusion
  230.7 0.5 broadcast_select_fusion.4
  (20 shorter events, 0.1 us)
Async XLA Ops:
  0.6 1.7 copy-start
  0.6 13.0 %copy-start.9 = (s32[128]{0:T(128)S(1)}, s32[128]{0:T(128)}, u32[]{:S(2)}) copy-start(s32[128]{0:T(128)} %param.16) | copy-start | bytes 1540
  6.5 93.7 %copy-start.10 = (bf16[512,288]{0,1:T(8,128)(2,1)S(1)}, bf16[512,288]{0,1:T(8,128)(2,1)}, u32[]{:S(2)}) copy-start(bf16[512,288]{0,1:T(8,128)(2,1)} %param.12) | copy-start | bytes 884740
  6.5 96.7 %all-to-all-start.1 = ((bf16[4,128,1152]{2,1,0:T(8,128)(2,1)}), bf16[4,128,1152]{2,1,0:T(8,128)(2,1)}, u32[]{:S(2)}, u32[]{:S(2)}) async-start(bf16[4,128,1152]{2,1,0:T(8,128)(2,1)} %bitcast.87), calls=%async_computation.1 | async-start | bytes 2359296 | tf_op jit(solution)/shard_map/all_to_all | solution.py:153
  103.2 7.3 %copy-start.3 = (bf16[128,1152]{1,0:T(8,128)(2,1)S(1)}, bf16[128,1152]{1,0:T(8,128)(2,1)}, u32[]{:S(2)}) copy-start(bf16[128,1152]{1,0:T(8,128)(2,1)} %param.11) | copy-start | bytes 884740
  103.2 28.7 %all-to-all-start = ((bf16[4,128,1152]{2,1,0:T(8,128)(2,1)}), bf16[4,128,1152]{2,1,0:T(8,128)(2,1)}, u32[]{:S(2)}, u32[]{:S(2)}) async-start(bf16[4,128,1152]{2,1,0:T(8,128)(2,1)} %bitcast.88), calls=%async_computation | async-start | bytes 2359296 | tf_op jit(solution)/shard_map/all_to_all | solution.py:153
  131.9 3.2 %copy-start.5 = (bf16[1,128,1152]{2,1,0:T(8,128)(2,1)S(1)}, bf16[1,128,1152]{2,1,0:T(8,128)(2,1)}, u32[]{:S(2)}) copy-start(bf16[1,128,1152]{2,1,0:T(8,128)(2,1)} %convert_bitcast_fusion) | copy-start | bytes 884740
  133.4 0.8 copy-start.1
  134.4 0.7 copy-start.4
  214.2 3.9 %copy-start.6 = (bf16[2,128,1152]{2,1,0:T(8,128)(2,1)S(1)}, bf16[2,128,1152]{2,1,0:T(8,128)(2,1)}, u32[]{:S(2)}) copy-start(bf16[2,128,1152]{2,1,0:T(8,128)(2,1)} %maximum_select_fusion.pay) | copy-start | bytes 1769476
  223.8 1.6 copy-start.8
  226.5 1.6 copy-start.2
  226.5 1.6 copy-start.7
where the time goes:
time: 232 us; the launch traced here: 231 us
  blocking collectives  84.9 us (37%)
  Pallas kernels  78.2 us (34%)
  waiting for transfers between devices  20.4 us (9%)
  matrix products  16.6 us (7%)
  starting transfers between devices  10.9 us (5%)
  other arithmetic  8.96 us (4%)
  local copies, waits for them, and re-layouts  8.38 us (4%)
  between operations  2.83 us (1%)
    all_gather x1, blocking collectives, gather_body(): lax.all_gather(match, both, axis=0, tiled=True).reshape(devices, rows)  84.9 us
    pallas_call x1, Pallas kernels, swap_blocks(): pl.pallas_call(exchange, out_shape=(jax.ShapeDtypeStruct((slots,) + block...  78.2 us
    all_to_all x2, waiting for transfers between devices, scatter_sum(): got = lax.all_to_all(pieces, axis, 0, 0).astype(jnp.float32)  20.4 us
    all_to_all x2, starting transfers between devices, scatter_sum(): got = lax.all_to_all(pieces, axis, 0, 0).astype(jnp.float32)  10.9 us
    dot_general x4, matrix products, part(): lax.dot_general(left, block, nt, preferred_element_type=jnp.float32)  4.8 us
    dot_general x4, matrix products, part(): jnp.dot(coef, block, preferred_element_type=jnp.float32)  4.7 us
  transfers between devices with their start and end apart: 2, of which 1 were waited for; matrix products, arithmetic and copies ran while one was open for 3% of the time, Pallas kernels for 0%

commit v1 on v0

v1 whole, which is shorter than its diff:
```python
import jax
import jax.numpy as jnp
from jax import lax
from jax.experimental import pallas as pl
from jax.experimental.pallas import tpu as pltpu
from jax.sharding import PartitionSpec as P

STEPS = 16


def shifted(shard, axis, by):
    devices = lax.axis_size(axis)
    return lax.ppermute(shard, axis, [(i, (i + by) % devices) for i in range(devices)])


def unit_rows(emb):
    length = jnp.sqrt(jnp.sum(emb * emb, axis=1, keepdims=True) + 1e-06)
    return (emb / length, length)


def pair_tile(image_low, text_block, owner, match, scale, shift_value):
    cosine = lax.dot_general(
        image_low, text_block, (((1,), (1,)), ((), ())), preferred_element_type=jnp.float32
    )
    text_index = owner * text_block.shape[0] + lax.iota(jnp.int32, text_block.shape[0])
    positive = match[:, None] == text_index[None, :]
    logit = scale * cosine + shift_value
    pair_loss = jnp.sum(
        jnp.where(positive, jax.nn.softplus(-logit), jax.nn.softplus(logit)), axis=1
    )
    coef = ((jax.nn.sigmoid(logit) - positive.astype(jnp.float32)) * scale).astype(jnp.bfloat16)
    image_part = jnp.dot(coef, text_block, preferred_element_type=jnp.float32)
    text_part = lax.dot_general(
        coef, image_low, (((0,), (0,)), ((), ())), preferred_element_type=jnp.float32
    )
    return (pair_loss, image_part, text_part)


def offset_blocks(blocks, window):
    windows = lax.axis_size(("dp", "tensor")) // STEPS
    for level in range((windows - 1).bit_length()):
        moved = shifted(blocks, ("dp", "tensor"), STEPS << level)
        blocks = jnp.where(window >> level & 1 == 1, moved, blocks)
    return blocks


def return_home(text_sum, fixed_steps, window):
    text_sum = shifted(text_sum, ("dp", "tensor"), -fixed_steps)
    windows = lax.axis_size(("dp", "tensor")) // STEPS
    for level in range((windows - 1).bit_length()):
        moved = shifted(text_sum, ("dp", "tensor"), -(STEPS << level))
        text_sum = jnp.where(window >> level & 1 == 1, moved, text_sum)
    return text_sum


def ring_body(
    img_hidden, img_down, img_pooled, txt_hidden, txt_proj, log_temp, bias, match, window_index
):
    width = img_pooled.shape[1]
    summed = lax.psum_scatter(
        jnp.concatenate(
            [
                jnp.dot(img_hidden, img_down, preferred_element_type=jnp.float32),
                jnp.dot(txt_hidden, txt_proj, preferred_element_type=jnp.float32),
            ],
            axis=1,
        ),
        "tensor",
        scatter_dimension=0,
        tiled=True,
    )
    img_emb = summed[:, :width] + img_pooled.astype(jnp.float32)
    txt_emb = summed[:, width:]
    img_unit, img_len = unit_rows(img_emb)
    txt_unit, txt_len = unit_rows(txt_emb)
    image_low = img_unit.astype(jnp.bfloat16)
    text_low = txt_unit.astype(jnp.bfloat16)
    scale = jnp.exp(log_temp[0])
    shift_value = bias[0]
    window = window_index[0]
    start_step = window * STEPS
    position = lax.axis_index(("dp", "tensor"))
    devices = lax.axis_size(("dp", "tensor"))
    half_steps = STEPS // 2
    late_copy = shifted(text_low, ("dp", "tensor"), STEPS - 1)
    stacked = offset_blocks(jnp.stack([text_low, late_copy]), window)
    early_block = stacked[0]
    late_block = stacked[1]
    early_owner = (position - start_step) % devices
    late_owner = (position - start_step - (STEPS - 1)) % devices
    early_loss, early_image, early_sum = pair_tile(
        image_low, early_block, early_owner, match, scale, shift_value
    )
    late_loss, late_image, late_sum = pair_tile(
        image_low, late_block, late_owner, match, scale, shift_value
    )

    def two_turn(turn, carry):
        early_now, late_now, early_acc, late_acc, image_now, loss_now = carry
        early_now = shifted(early_now, ("dp", "tensor"), 1)
        late_now = shifted(late_now, ("dp", "tensor"), -1)
        early_acc = shifted(early_acc, ("dp", "tensor"), 1)
        late_acc = shifted(late_acc, ("dp", "tensor"), -1)
        owner_early = (position - start_step - turn) % devices
        owner_late = (position - start_step - (STEPS - 1) + turn) % devices
        loss_one, image_one, text_one = pair_tile(
            image_low, early_now, owner_early, match, scale, shift_value
        )
        loss_two, image_two, text_two = pair_tile(
            image_low, late_now, owner_late, match, scale, shift_value
        )
        return (
            early_now,
            late_now,
            early_acc + text_one,
            late_acc + text_two,
            image_now + image_one + image_two,
            loss_now + loss_one + loss_two,
        )

    carried = lax.fori_loop(
        1,
        half_steps,
        two_turn,
        (
            early_block,
            late_block,
            early_sum,
            late_sum,
            early_image + late_image,
            early_loss + late_loss,
        ),
    )
    early_sum = carried[2]
    late_sum = carried[3]
    image_dunit = carried[4]
    row_loss = carried[5]
    late_moved = shifted(late_sum, ("dp", "tensor"), -1)
    text_dunit = return_home(early_sum + late_moved, half_steps - 1, window)
    img_grad = (
        image_dunit - img_unit * jnp.sum(img_unit * image_dunit, axis=1, keepdims=True)
    ) / img_len
    txt_grad = (
        text_dunit - txt_unit * jnp.sum(txt_unit * text_dunit, axis=1, keepdims=True)
    ) / txt_len
    return (img_grad, txt_grad, row_loss)


def tangent(dunit, unit, inverse):
    return (dunit - unit * jnp.sum(unit * dunit, axis=1, keepdims=True)) * inverse


def unit_low(emb):
    inverse = 1.0 / jnp.sqrt(jnp.sum(emb * emb, axis=1, keepdims=True) + 1e-06)
    return emb * inverse, inverse


def stable_terms(logit, positive):
    signed = jnp.where(positive, -logit, logit)
    small = jnp.exp(-jnp.abs(signed))
    loss = jnp.maximum(signed, 0.0) + jnp.log1p(small)
    chance = jnp.where(signed >= 0.0, 1.0, small) / (1.0 + small)
    return loss, jnp.where(positive, -chance, chance)


HALVES = 2
TAIL = 32


def plane_kernel(
    log_temp,
    bias,
    window_index,
    match,
    acts,
    txt_proj,
    img_hidden,
    img_down,
    img_pooled,
    img_grad,
    txt_grad,
    row_loss,
    acts_all,
    weights,
    hidden,
    down,
    pooled,
    partial,
    chain_out,
    chain_in,
    img_all,
    img_unit,
    img_inv,
    txt_low,
    txt_unit,
    txt_inv,
    coef_all,
    match_all,
    loss_out,
    loss_in,
    tg_own,
    tg_out,
    tg_in,
    even,
    cross_out,
    cross_in,
    plane_out,
    plane_in,
    loc_sem,
    a_send,
    a_recv,
    w_zsend,
    w_psend,
    w_csend,
    w_recv,
    m_send,
    m_recv,
    c_send,
    c_recv,
    i_send,
    i_fsend,
    i_recv,
    t_send,
    t_recv,
    x_send,
    x_recv,
    p_send,
    p_recv,
    l_send,
    l_recv,
):
    mesh_id = pl.DeviceIdType.MESH
    dp = lax.axis_index("dp")
    z = lax.axis_index("tensor")
    groups = lax.axis_size("dp")
    depth = lax.axis_size("tensor")
    chips = groups // 2
    rows = img_pooled.shape[0]
    width = img_pooled.shape[1]
    piece = rows // HALVES
    chip = dp // 2
    c = dp % 2
    partner = chip * 2 + 1 - c
    y, x = chip // 2, chip % 2
    near = [
        (y * 2 + 1 - x) * 2 + c,
        ((1 - y) * 2 + x) * 2 + c,
        ((1 - y) * 2 + 1 - x) * 2 + c,
    ]
    part_rows = weights.shape[1] // chips
    features = txt_proj.shape[0]
    main = features - TAIL

    local = [
        pltpu.make_async_copy(acts, acts_all.at[z], loc_sem.at[0]),
        pltpu.make_async_copy(txt_proj, weights.at[z, pl.ds(0, features)], loc_sem.at[1]),
        pltpu.make_async_copy(img_hidden, hidden, loc_sem.at[2]),
        pltpu.make_async_copy(img_down, down, loc_sem.at[3]),
        pltpu.make_async_copy(img_pooled, pooled, loc_sem.at[4]),
    ]
    for copy in local:
        copy.start()
    weights[z, pl.ds(features, weights.shape[1] - features)] = jnp.zeros(
        (weights.shape[1] - features, width), weights.dtype
    )

    barrier = pltpu.get_barrier_semaphore()
    for ahead in range(1, groups):
        pl.semaphore_signal(
            barrier, inc=1, device_id=((dp + ahead) % groups, z), device_id_type=mesh_id
        )
    for ahead in range(1, depth):
        pl.semaphore_signal(
            barrier, inc=1, device_id=(dp, (z + ahead) % depth), device_id_type=mesh_id
        )
    pl.semaphore_wait(barrier, groups + depth - 2)

    started = []

    def send(source, target, send_sem, recv_sem, device, when=None):
        def make():
            return pltpu.make_async_remote_copy(
                src_ref=source,
                dst_ref=target,
                send_sem=send_sem,
                recv_sem=recv_sem,
                device_id=device,
                device_id_type=mesh_id,
            )

        if when is None:
            make().start()
        else:

            @pl.when(when)
            def _():
                make().start()

        started.append((when, make))

    def arrive(target, recv_sem):
        pltpu.make_async_remote_copy(
            src_ref=target,
            dst_ref=target,
            send_sem=loc_sem.at[0],
            recv_sem=recv_sem,
            device_id=(partner, z),
            device_id_type=mesh_id,
        ).wait_recv()

    def arrive_when(when, target, recv_sem):
        @pl.when(when)
        def _():
            arrive(target, recv_sem)

    has_up = z < depth - 1
    has_down = z > 0

    local[0].wait()
    send(acts_all.at[z], acts_all.at[z], a_send.at[0, 0], a_recv.at[z], (dp, z + 1), has_up)
    send(acts_all.at[z], acts_all.at[z], a_send.at[1, 0], a_recv.at[z], (dp, z - 1), has_down)
    local[1].wait()
    flow = 1 - 2 * c
    flow_on = jnp.logical_and(z + flow >= 0, z + flow < depth)

    def part(level, index):
        start = pl.multiple_of(index * part_rows, part_rows)
        return weights.at[level, pl.ds(start, part_rows)]

    send(part(z, chip), part(z, chip), w_zsend.at[0], w_recv.at[z, chip], (dp, z + flow), flow_on)
    for ahead in range(1, groups):
        send(
            match,
            match_all.at[dp],
            m_send.at[ahead],
            m_recv.at[dp],
            ((dp + ahead) % groups, z),
        )
    match_all[dp] = match[...]

    upper = z // (depth // 2)
    toward = 1 - 2 * upper
    is_end = jnp.logical_or(z == 0, z == depth - 1)
    is_inner = jnp.logical_not(is_end)

    def mirror(level):
        return level + upper * (depth - 1 - 2 * level)

    local[2].wait()
    local[3].wait()
    local[4].wait()
    for step in range(depth):
        block = mirror(depth - 1 - step)
        partial[block] = jnp.dot(
            hidden[pl.ds(pl.multiple_of(block * rows, rows), rows), :],
            down[...],
            preferred_element_type=jnp.float32,
        )
        if step < depth - 1:

            @pl.when(is_end)
            def _(block=block):
                chain_out[upper, block] = partial[block].astype(chain_out.dtype)

            for h in range(HALVES):
                span = pl.ds(h * piece, piece)
                send(
                    chain_out.at[upper, block, span],
                    chain_in.at[upper, block, span],
                    c_send.at[upper, block, h],
                    c_recv.at[upper, block, h],
                    (dp, z + toward),
                    is_end,
                )

    def spread_weights(hop):
        level = z - flow * hop
        here = jnp.logical_and(level >= 0, level < depth)

        @pl.when(here)
        def _():
            arrive(part(level, chip), w_recv.at[level, chip])

        send(
            part(level, chip),
            part(level, chip),
            w_zsend.at[hop],
            w_recv.at[level, chip],
            (dp, z + flow),
            jnp.logical_and(here, flow_on),
        )
        for job, peer in enumerate(near):
            send(
                part(level, chip),
                part(level, chip),
                w_psend.at[hop, job],
                w_recv.at[level, chip],
                (peer, z),
                here,
            )
        send(
            part(level, chip),
            part(level, chip),
            w_csend.at[hop, 0],
            w_recv.at[level, chip],
            (partner, z),
            here,
        )

    def relay_acts(tag, level, way, forward):
        arrive(acts_all.at[level], a_recv.at[level])
        if forward:
            pltpu.make_async_remote_copy(
                src_ref=acts_all.at[level],
                dst_ref=acts_all.at[level],
                send_sem=a_send.at[way, tag],
                recv_sem=a_recv.at[level],
                device_id=(dp, z + (toward if way == 0 else -toward)),
                device_id_type=mesh_id,
            ).start()

    def relay_sums(block, way):
        lane = upper if way == 0 else 1 - upper
        for h in range(HALVES):
            span = pl.ds(h * piece, piece)
            arrive(chain_in.at[lane, block, span], c_recv.at[lane, block, h])
            chain_out[lane, block, span] = (
                partial[block, span] + chain_in[lane, block, span].astype(jnp.float32)
            ).astype(chain_out.dtype)
            pltpu.make_async_remote_copy(
                src_ref=chain_out.at[lane, block, span],
                dst_ref=chain_in.at[lane, block, span],
                send_sem=c_send.at[lane, block, h],
                recv_sem=c_recv.at[lane, block, h],
                device_id=(dp, z + (toward if way == 0 else -toward)),
                device_id_type=mesh_id,
            ).start()

    def sent(source, send_sem):
        pltpu.make_async_remote_copy(
            src_ref=source,
            dst_ref=source,
            send_sem=send_sem,
            recv_sem=loc_sem.at[0],
            device_id=(partner, z),
            device_id_type=mesh_id,
        ).wait_send()

    m0, m1, m2, m3 = (mirror(level) for level in range(4))
    spread_weights(1)

    @pl.when(is_inner)
    def _():
        relay_acts(1, m0, 0, True)
        relay_acts(1, m2, 1, True)

    spread_weights(2)

    @pl.when(is_inner)
    def _():
        relay_sums(m3, 0)
        relay_acts(2, m3, 1, True)

    spread_weights(3)

    @pl.when(is_inner)
    def _():
        relay_sums(m2, 0)
        relay_sums(m0, 1)

    @pl.when(is_end)
    def _():
        for level in (m1, m2, m3):
            relay_acts(0, level, 0, False)

    for h in range(HALVES):
        span = pl.ds(h * piece, piece)
        from_far = chain_in.at[1 - upper, z, span]
        from_near = chain_in.at[upper, z, span]
        arrive(from_far, c_recv.at[1 - upper, z, h])
        partial[z, span] = partial[z, span] + chain_in[1 - upper, z, span].astype(jnp.float32)

        @pl.when(is_inner)
        def _():
            arrive(from_near, c_recv.at[upper, z, h])
            partial[z, span] = partial[z, span] + chain_in[upper, z, span].astype(jnp.float32)

        unit, inverse = unit_low(partial[z, span] + pooled[span].astype(jnp.float32))
        img_unit[span] = unit
        img_inv[span] = inverse
        img_all[dp, span] = unit.astype(img_all.dtype)
        for job, peer in enumerate(near + [partner]):
            send(
                img_all.at[dp, span],
                img_all.at[dp, span],
                i_send.at[h, job],
                i_recv.at[dp, h],
                (peer, z),
            )

    for hop in range(1, depth):
        level = z - flow * hop
        here = jnp.logical_and(level >= 0, level < depth)
        for job, peer in enumerate(near):
            index = peer // 2
            arrive_when(here, part(level, index), w_recv.at[level, index])
            send(
                part(level, index),
                part(level, index),
                w_csend.at[hop, 1 + job],
                w_recv.at[level, index],
                (partner, z),
                here,
            )
    for hop in range(1, depth):
        level = z + flow * hop
        here = jnp.logical_and(level >= 0, level < depth)
        for index in range(chips):
            arrive_when(here, part(level, index), w_recv.at[level, index])

    lanes = lax.broadcasted_iota(jnp.int32, (rows // 2, main), 1) // TAIL
    repeats = main // TAIL
    for off in range(depth):
        block = (z + off) % depth
        emb = jnp.zeros((rows, width), jnp.float32)
        tails = [jnp.zeros((rows // 2, width), jnp.float32) for _ in range(2)]
        for level in range(depth):
            emb += jnp.dot(
                acts_all[level, pl.ds(pl.multiple_of(block * rows, rows), rows)],
                weights[level, pl.ds(0, main)],
                preferred_element_type=jnp.float32,
            )
            packed = acts_all[level, pl.ds(depth * rows, rows // 2)]
            tail = jnp.concatenate([weights[level, pl.ds(main, TAIL)]] * repeats, axis=0)
            for s in range(2):
                tails[s] += jnp.dot(
                    jnp.where(lanes == 2 * block + s, packed, jnp.zeros_like(packed)),
                    tail,
                    preferred_element_type=jnp.float32,
                )
        unit, inverse = unit_low(emb + jnp.concatenate(tails, axis=0))
        txt_low[pl.ds(off * rows, rows)] = unit.astype(txt_low.dtype)
        if off == 0:
            txt_unit[...] = unit
            txt_inv[...] = inverse

    for h in range(HALVES):
        span = pl.ds(h * piece, piece)
        for job, peer in enumerate(near):
            arrive(img_all.at[peer, span], i_recv.at[peer, h])
            send(
                img_all.at[peer, span],
                img_all.at[peer, span],
                i_fsend.at[h, job],
                i_recv.at[peer, h],
                (partner, z),
            )
    for h in range(HALVES):
        span = pl.ds(h * piece, piece)
        for peer in [partner] + [2 * (p // 2) + 1 - c for p in near]:
            arrive(img_all.at[peer, span], i_recv.at[peer, h])
    for ahead in range(1, groups):
        peer = (dp + ahead) % groups
        arrive(match_all.at[peer], m_recv.at[peer])

    scale = jnp.exp(jnp.full((rows, rows), log_temp[0], jnp.float32))
    shift_value = bias[0]
    window = window_index[0]
    half_groups = groups // 2
    nt = (((1,), (1,)), ((), ()))
    tn = (((0,), (0,)), ((), ()))
    losses = [jnp.zeros((1, rows), jnp.float32) for _ in range(half_groups + 1)]
    for off in (2, 1, 3, 0):
        block = (z + off) % depth
        here = txt_low[pl.ds(off * rows, rows)]
        text_index = (dp * depth + block) * rows + lax.broadcasted_iota(
            jnp.int32, (rows, rows), 0
        )
        beyond = (block > z).astype(jnp.int32)
        far = beyond + window - 2 * beyond * window
        total = jnp.zeros((rows, width), jnp.float32)
        for slot in range(half_groups):
            jump = half_groups * far if slot == 0 else slot + half_groups * window
            who = (dp + jump) % groups
            image = img_all[who]
            cosine = lax.dot_general(here, image, nt, preferred_element_type=jnp.float32)
            logit = scale * cosine + shift_value
            loss, slope = stable_terms(logit, match_all[who] == text_index)
            coef = (slope * scale).astype(jnp.bfloat16)
            total += jnp.dot(coef, image, preferred_element_type=jnp.float32)
            lost = jnp.sum(loss, axis=0, keepdims=True)
            if slot:
                coef_all[slot, pl.ds(off * rows, rows)] = coef
                losses[slot] += lost
            else:
                zero = jnp.zeros_like(coef)
                coef_all[0, pl.ds(off * rows, rows)] = jnp.where(far == 0, coef, zero)
                coef_all[half_groups, pl.ds(off * rows, rows)] = jnp.where(far == 1, coef, zero)
                losses[0] += jnp.where(far == 0, lost, 0.0)
                losses[half_groups] += jnp.where(far == 1, lost, 0.0)
        if off:
            tg_out[off] = total.astype(tg_out.dtype)
            send(tg_out.at[off], tg_in.at[off], t_send.at[off], t_recv.at[off], (dp, block))
        else:
            tg_own[...] = total

    first = window == 0
    for jump in range(groups):
        if jump % half_groups == 0:
            value = losses[jump]
        else:
            value = jnp.where(first if jump < half_groups else window == 1, losses[jump % half_groups], 0.0)
        loss_out[jump] = value
    for jump in range(1, groups):
        send(
            loss_out.at[jump],
            loss_in.at[jump],
            l_send.at[jump],
            l_recv.at[jump],
            ((dp + jump) % groups, z),
        )

    def image_sum(slot):
        return lax.dot_general(
            coef_all[slot], txt_low[...], tn, preferred_element_type=jnp.float32
        )

    for slot in (1, 3):
        value = image_sum(slot)
        for late in (0, 1):
            lane = ((slot - 1) // 2 + 2 * late + c) % chips
            kept = jnp.where(window == late, value, 0.0)
            cross_out[lane] = kept.astype(cross_out.dtype)
            send(
                cross_out.at[lane],
                cross_in.at[lane],
                x_send.at[lane],
                x_recv.at[lane],
                (partner, z),
            )
    value = image_sum(2)
    even[1] = jnp.where(window == 0, value, 0.0)
    even[3] = jnp.where(window == 1, value, 0.0)
    even[2] = image_sum(half_groups)
    even[0] = image_sum(0)
    for lane in (1, 2, 3):
        arrive(cross_in.at[lane], x_recv.at[lane])
        plane_out[lane] = (even[lane] + cross_in[lane].astype(jnp.float32)).astype(plane_out.dtype)
        send(
            plane_out.at[lane],
            plane_in.at[lane],
            p_send.at[lane],
            p_recv.at[lane],
            (((chip + lane) % chips) * 2 + c, z),
        )
    arrive(cross_in.at[0], x_recv.at[0])
    dunit = even[0] + cross_in[0].astype(jnp.float32)
    total = loss_out[0]
    for jump in range(1, groups):
        arrive(loss_in.at[jump], l_recv.at[jump])
        total += loss_in[jump]
    row_loss[...] = total
    for lane in (1, 2, 3):
        arrive(plane_in.at[lane], p_recv.at[lane])
        dunit += plane_in[lane].astype(jnp.float32)
    img_grad[...] = tangent(dunit, img_unit[...], img_inv[...])
    dunit = tg_own[...]
    for off in (1, 2, 3):
        arrive(tg_in.at[off], t_recv.at[off])
        dunit += tg_in[off].astype(jnp.float32)
    txt_grad[...] = tangent(dunit, txt_unit[...], txt_inv[...])

    for when, make in started:
        if when is None:
            make().wait_send()
        else:

            @pl.when(when)
            def _():
                make().wait_send()

    @pl.when(is_inner)
    def _():
        sent(acts_all.at[m0], a_send.at[0, 1])
        sent(acts_all.at[m2], a_send.at[1, 1])
        sent(acts_all.at[m3], a_send.at[1, 2])
        for block, way in ((m3, 0), (m2, 0), (m0, 1)):
            lane = upper if way == 0 else 1 - upper
            for h in range(HALVES):
                span = pl.ds(h * piece, piece)
                sent(chain_out.at[lane, block, span], c_send.at[lane, block, h])


def plane_body(
    img_hidden, img_down, img_pooled, txt_hidden, txt_proj, log_temp, bias, match, window_index
):
    groups = lax.axis_size("dp")
    depth = lax.axis_size("tensor")
    chips = groups // 2
    rows, width = img_pooled.shape
    features = txt_hidden.shape[1]
    main = features - TAIL
    fold = main // TAIL
    packed = (
        txt_hidden[:, main:]
        .reshape(fold, depth * rows // fold, TAIL)
        .transpose(1, 0, 2)
        .reshape(depth * rows // fold, main)
    )
    acts = jnp.concatenate([txt_hidden[:, :main], packed], axis=0)
    padded = -(-features // (16 * chips)) * 16 * chips
    dma = pltpu.SemaphoreType.DMA
    low, full = jnp.bfloat16, jnp.float32
    vmem = pltpu.VMEM
    smem = pl.BlockSpec(memory_space=pltpu.SMEM)
    inside = pl.BlockSpec(memory_space=pltpu.VMEM)
    anywhere = pl.BlockSpec(memory_space=pl.ANY)
    block = (rows, width)
    img_grad, txt_grad, row_loss = pl.pallas_call(
        plane_kernel,
        out_shape=(
            jax.ShapeDtypeStruct(block, full),
            jax.ShapeDtypeStruct(block, full),
            jax.ShapeDtypeStruct((1, rows), full),
        ),
        in_specs=[smem, smem, smem, inside] + [anywhere] * 5,
        out_specs=(inside, inside, inside),
        scratch_shapes=[
            vmem((depth,) + acts.shape, low),
            vmem((depth, padded, width), low),
            vmem(img_hidden.shape, low),
            vmem(img_down.shape, low),
            vmem(block, low),
            vmem((depth,) + block, full),
            vmem((2, depth) + block, low),
            vmem((2, depth) + block, low),
            vmem((groups,) + block, low),
            vmem(block, full),
            vmem((rows, 1), full),
            vmem((depth * rows, width), low),
            vmem(block, full),
            vmem((rows, 1), full),
            vmem((groups // 2 + 1, depth * rows, rows), low),
            vmem((groups, 1, rows), jnp.int32),
            vmem((groups, 1, rows), full),
            vmem((groups, 1, rows), full),
            vmem(block, full),
            vmem((depth,) + block, low),
            vmem((depth,) + block, low),
            vmem((chips,) + block, full),
            vmem((chips,) + block, low),
            vmem((chips,) + block, low),
            vmem((chips,) + block, low),
            vmem((chips,) + block, low),
            dma((5,)),
            dma((2, depth)),
            dma((depth,)),
            dma((depth,)),
            dma((depth, 3)),
            dma((depth, 4)),
            dma((depth, chips)),
            dma((groups,)),
            dma((groups,)),
            dma((2, depth, HALVES)),
            dma((2, depth, HALVES)),
            dma((HALVES, 4)),
            dma((HALVES, 3)),
            dma((groups, HALVES)),
            dma((depth,)),
            dma((depth,)),
            dma((chips,)),
            dma((chips,)),
            dma((chips,)),
            dma((chips,)),
            dma((groups,)),
            dma((groups,)),
        ],
        compiler_params=pltpu.CompilerParams(
            collective_id=1, has_side_effects=True, vmem_limit_bytes=60 * 1024 * 1024
        ),
        name="plane",
    )(
        log_temp,
        bias,
        window_index,
        match.reshape(1, rows),
        acts,
        txt_proj,
        img_hidden,
        img_down,
        img_pooled,
    )
    return img_grad, txt_grad, row_loss.reshape(rows)


def solution(mesh):
    in_specs = (
        P("dp", "tensor"),
        P("tensor", None),
        P(("dp", "tensor"), None),
        P("dp", "tensor"),
        P("tensor", None),
        P(),
        P(),
        P(("dp", "tensor")),
        P(),
    )
    out_specs = (P(("dp", "tensor"), None), P(("dp", "tensor"), None), P(("dp", "tensor")))
    whole = mesh.shape["dp"] * mesh.shape["tensor"]
    body = plane_body if whole == 2 * STEPS and mesh.shape["dp"] == 8 and mesh.shape["tensor"] == 4 else ring_body
    return jax.shard_map(body, mesh=mesh, in_specs=in_specs, out_specs=out_specs, check_vma=False)
```

time: 232 us -> 93.1 us (0.40)
  the two profiles are of different devices: /device:TPU:0 before, /device:TPU:17 now
where the time goes in v1:
time: 93.1 us; the launch traced here: 92.8 us
  Pallas kernels  82.6 us (89%)
  local copies, waits for them, and re-layouts  6.79 us (7%)
  between operations  2.72 us (3%)
    pallas_call x1, Pallas kernels, plane_body(): pl.pallas_call(plane_kernel, out_shape=(jax.ShapeDtypeStruct(block, full)...  82.6 us
    unnamed x11, local copies, waits for them, and re-layouts  4.85 us

profile of v1, /device:TPU:17, one launch (start us, length us, event | category | flops | bytes accessed | tf_op | source)
XLA Modules:
  0.0 92.8 jit_solution(4485263743289798012)
XLA Ops:
  0.6 0.0 copy-start
  2.7 0.8 slice.7
  3.4 0.1 reshape.19
  3.6 0.1 copy.17
  3.7 1.0 %slice.6 = bf16[512,256]{0,1:T(8,128)(2,1)S(1)} slice(bf16[512,288]{0,1:T(8,128)(2,1)} %param.12), slice={[0:512], [0:256]} | slice | bytes 524288 | tf_op jit(solution)/shard_map/slice | solution.py:710
  4.6 0.1 copy.19
  4.8 0.7 pad_maximum_fusion.acts
  5.5 0.0 copy-done
  5.5 1.4 %copy.18.img_hidden = bf16[512,1076]{1,0:T(8,128)(2,1)} copy(bf16[512,1076]{0,1:T(8,128)(2,1)S(1)} %copy-done) | data formatting | bytes 2203648 | tf_op args[0]
  6.9 82.6 %plane.1 = (f32[128,1152]{1,0:T(8,128)}, f32[128,1152]{1,0:T(8,128)}, f32[1,128]{1,0:T(1,128)}) custom-call(f32[1]{0:T(128)S(6)} %copy.23.log_temp, f32[1]{0:T(128)S(6)} %copy.24.bias, s32[1]{0:T(128)S(6)} %copy.25.window_index, s32[1,128]{1,0:T(1,128)} %bitcast.8, bf16[576,256]{1,0:T(8,128)(2,1)} %pad_maximum_fusion.acts, bf16[288,1152]{1,0:T(8,128)(2,1)} %txt_proj.1, ...), custom_call_target="tpu_custom_call" | custom-call | tf_op jit(solution)/shard_map/plane/pallas_call | solution.py:719
  89.5 0.0 copy-start.1
  89.5 0.0 copy-start.2
  89.5 2.0 %copy.26 = f32[128,1152]{1,0:T(8,128)} copy(f32[128,1152]{1,0:T(8,128)} %get-tuple-element.12) | data formatting | bytes 1179648
  91.5 0.0 copy-done.1
  91.5 0.8 copy.27
  92.3 0.0 copy-done.2
  92.3 0.5 copy.28
  (1 shorter events, 0.0 us)
Async XLA Ops:
  0.6 4.9 %copy-start = (bf16[512,1076]{0,1:T(8,128)(2,1)S(1)}, bf16[512,1076]{0,1:T(8,128)(2,1)}, u32[]{:S(2)}) copy-start(bf16[512,1076]{0,1:T(8,128)(2,1)} %param.9) | copy-start | bytes 3305476
  89.5 2.0 %copy-start.1 = (f32[128,1152]{1,0:T(8,128)S(1)}, f32[128,1152]{1,0:T(8,128)}, u32[]{:S(2)}) copy-start(f32[128,1152]{1,0:T(8,128)} %get-tuple-element.13) | copy-start | bytes 1769476
  89.5 2.8 %copy-start.2 = (f32[1,128]{1,0:T(1,128)S(1)}, f32[1,128]{1,0:T(1,128)}, u32[]{:S(2)}) copy-start(f32[1,128]{1,0:T(1,128)} %get-tuple-element.8) | copy-start | bytes 1540
